TPU v7x, 32 devices: a whole 2x2x4 slice. The times are simulated.
32 devices in a mesh: dp: 8 (over z, core), mp: 4 (over y, x).
Axes of the slice: x: 2, y: 2, z: 4, core: 2. Of those that a mesh axis runs over, the one named last changes fastest.
Arguments:
- token_ids: int32 [8192], P('dp'), may hold values from 0 to 128255
- lengths: int32 [64], P('dp'), may hold values from 1 to 128
- embed_grads: bfloat16 [8192, 4096], P('dp', 'mp'), may hold values from -6 to 6
- vocab_basis: bfloat16 [128256, 32], P('mp'), may hold values from -6 to 6
- embed_basis: bfloat16 [4096, 32], P('mp'), may hold values from -0.09375 to 0.09375
- layer_inputs: bfloat16 [1, 8192, 4096], P(None, 'dp', 'mp'), may hold values from -6 to 6
- layer_grads: bfloat16 [1, 8192, 4096], P(None, 'dp', 'mp'), may hold values from -6 to 6
- input_basis: bfloat16 [1, 4096, 32], P(None, 'mp'), may hold values from -0.09375 to 0.09375
- output_basis: bfloat16 [1, 4096, 32], P(None, 'mp'), may hold values from -0.09375 to 0.09375
- queries: bfloat16 [2, 1024, 256], P(None, 'mp', 'dp'), may hold values from -0.19921875 to 0.19921875
Outputs:
- scores: float32 [64, 256], P('dp')
All inputs are finite; a program needn't handle non-finite values.
Results may differ from a plain program's by a relative error of at most 0.0003.
Values may be sent and summed in bfloat16 or wider, within the bound.
No kernel may reach another device: no remote copies, remote signals or barrier semaphores. Data moves between devices by JAX's collectives and lax.ppermute only.
A program may use at most 64 MiB of HBM per device.

v0:
```python
import jax
import jax.numpy as jnp
from jax import lax
from jax.sharding import PartitionSpec as P

ITERS = 2
damping = 0.01
epsilon = 1e-06
highest = lax.Precision.HIGHEST


def solve_columns(right_side, apply_operator, column_norm, column_curve):
    solution = jnp.zeros_like(right_side)
    residual = right_side
    direction = right_side
    norm_now = column_norm(residual)
    for iteration in range(ITERS):
        images = apply_operator(direction)
        step_size = norm_now / (column_curve(direction, images) + epsilon)
        solution = solution + step_size[:, None, :] * direction
        residual = residual - step_size[:, None, :] * images
        norm_next = column_norm(residual)
        direction = residual + (norm_next / (norm_now + epsilon))[:, None, :] * direction
        norm_now = norm_next
    return solution


def per_device(
    token_ids,
    lengths,
    embed_grads,
    vocab_basis,
    embed_basis,
    layer_inputs,
    layer_grads,
    input_basis,
    output_basis,
    queries,
):
    vocab_rows = vocab_basis.shape[0]
    basis_rank = embed_basis.shape[1]
    layer_count = layer_inputs.shape[0] + 1
    seq_count = lengths.shape[0]
    token_count = token_ids.shape[0]
    slot_len = token_count // seq_count
    sketch_len = basis_rank * basis_rank
    mp_index = lax.axis_index("mp")
    local_ids = token_ids - mp_index * vocab_rows
    inside = (local_ids >= 0) & (local_ids < vocab_rows)
    looked = jnp.take(vocab_basis, jnp.clip(local_ids, 0, vocab_rows - 1), axis=0)
    pieces = [
        jnp.dot(embed_grads, embed_basis, preferred_element_type=jnp.float32),
        jnp.where(inside[:, None], looked.astype(jnp.float32), 0.0),
    ]
    pieces.append(jnp.dot(layer_grads[0], output_basis[0], preferred_element_type=jnp.float32))
    pieces.append(jnp.dot(layer_inputs[0], input_basis[0], preferred_element_type=jnp.float32))
    projected = jnp.concatenate(pieces, axis=1)
    inverse_len = 1.0 / lengths.astype(jnp.float32)
    summed = lax.psum(projected, "mp")
    layout = summed.reshape(seq_count, slot_len, layer_count, 2, basis_rank)
    position = jnp.arange(slot_len, dtype=jnp.int32)
    weights = jnp.where(position[None, :] < lengths[:, None], inverse_len[:, None], 0.0)
    weighted = layout[:, :, :, 0, :] * weights[:, :, None, None]
    sketches = jnp.einsum(
        "stli,stlj->lsij", weighted, layout[:, :, :, 1, :], precision=highest
    ).reshape(layer_count, seq_count, sketch_len)
    examples = seq_count * lax.axis_size("dp")
    targets = lax.all_gather(queries, "dp", axis=2, tiled=True)
    everyone = lax.all_gather(sketches, "dp", axis=1, tiled=True)
    columns = lax.all_to_all(targets, "mp", split_axis=2, concat_axis=1, tiled=True)

    def apply_sketch(direction):
        inner_sums = jnp.einsum("lek,lkq->leq", everyone, direction, precision=highest)
        back_proj = jnp.einsum("lek,leq->lkq", everyone, inner_sums, precision=highest)
        return back_proj / examples + damping * direction

    def local_norm(residual):
        return jnp.sum(residual * residual, axis=1)

    def local_curve(direction, images):
        return jnp.sum(direction * images, axis=1)

    solution = solve_columns(columns.astype(jnp.float32), apply_sketch, local_norm, local_curve)
    partial_value = jnp.einsum("lek,lkq->eq", sketches, solution, precision=highest)
    scores = lax.all_gather(partial_value, "mp", axis=1, tiled=True)
    return scores


def solution(mesh):
    placed = (
        P("dp"),
        P("dp"),
        P("dp", "mp"),
        P("mp", None),
        P("mp", None),
        P(None, "dp", "mp"),
        P(None, "dp", "mp"),
        P(None, "mp", None),
        P(None, "mp", None),
        P(None, "mp", "dp"),
    )
    return jax.shard_map(
        per_device, mesh=mesh, in_specs=placed, out_specs=P("dp", None), check_vma=False
    )
```

profile of v0, /device:TPU:0, one launch (start us, length us, event | category | flops | bytes accessed | tf_op | source)
XLA Modules:
  0.0 111.8 jit_solution(4883537781208353662)
XLA Ops:
  6.5 0.0 copy-start
  6.5 0.0 all-reduce.2.cloned.1.call-start
  6.5 0.8 compare_and_fusion.1
  7.4 0.7 fusion.25
  8.1 7.3 %copy.30 = bf16[32064,32]{1,0:T(8,128)(2,1)} copy(bf16[32064,32]{0,1:T(8,128)(2,1)} %param.13) | data formatting | bytes 4104192 | tf_op args[3]
  15.4 0.0 copy-start.3
  15.4 0.0 copy-start.4
  15.4 7.3 %gather_fusion = bf16[1024,32]{1,0:T(8,128)(2,1)S(1)} fusion(bf16[32064,32]{1,0:T(8,128)(2,1)} %copy.30, s32[1024]{0:T(1024)S(1)} %fusion.25), kind=kCustom, calls=%fused_computation | custom fusion | bytes 135168 | tf_op jit(solution)/shard_map/jit(_take)/gather | solution.py:50
  22.7 0.1 copy.31
  22.8 0.0 copy-done
  22.8 0.0 copy-done.3
  22.8 0.0 copy-start.1
  22.8 0.0 copy-start.2
  22.8 0.0 copy-start.5
  22.8 0.7 fusion
  23.6 0.0 copy-done.4
  23.6 0.8 copy-done.1
  24.4 0.7 fusion.2
  25.1 0.0 copy-done.2
  25.1 0.0 copy-done.5
  25.1 0.7 fusion.26
  25.9 0.0 copy-start.6
  25.9 0.0 copy-start.7
  26.0 0.1 copy.38
  26.1 0.9 copy.32
  27.0 0.0 all-reduce.2.cloned.1.call-update
  27.0 0.0 copy-done.6
  27.0 17.0 %all_gather.9 = bf16[2,256,256]{1,0,2:T(2,128)(2,1)} all-gather(bf16[2,256,32]{1,0,2:T(2,128)(2,1)S(1)} %copy.28), channel_id=1, replica_groups=mesh['dp'=8,'mp'=4] {'dp'}, dimensions={2}, use_global_device_ids=true | all-gather | bytes 294912 | tf_op jit(solution)/shard_map/all_gather | solution.py:68
  44.0 3.7 %all-to-all-start = ((bf16[2,256,256]{1,0,2:T(2,128)(2,1)}), bf16[2,256,256]{1,0,2:T(2,128)(2,1)S(1)}, u32[]{:S(2)}, u32[]{:S(2)}) async-start(bf16[2,256,256]{1,0,2:T(2,128)(2,1)} %all_gather.9), calls=%async_computation | async-start | bytes 524288 | tf_op jit(solution)/shard_map/all_to_all | solution.py:70
  47.7 0.0 copy-done.7
  47.8 0.1 fusion.24
  47.8 5.8 %all-to-all-done = bf16[2,256,256]{1,0,2:T(2,128)(2,1)S(1)} async-done(((bf16[2,256,256]{1,0,2:T(2,128)(2,1)}), bf16[2,256,256]{1,0,2:T(2,128)(2,1)S(1)}, u32[]{:S(2)}, u32[]{:S(2)}) %all-to-all-start) | async-done | bytes 262176 | tf_op jit(solution)/shard_map/all_to_all | solution.py:70
  53.6 0.2 copy.42
  53.8 0.2 all_to_all.16
  54.0 0.6 multiply_reduce_fusion.1
  54.6 21.5 %all-reduce.2.cloned.1.call-done = f32[8,128,2,2,32]{1,4,0,2,3:T(8,128)} async-done(((f32[8,128,2,2,32]{1,4,0,2,3:T(8,128)}), f32[8,128,2,2,32]{1,4,0,2,3:T(8,128)}) %all-reduce.2.cloned.1.call-update) | async-done | bytes 524304 | tf_op jit(solution)/shard_map/psum | solution.py:59
  76.0 1.6 %fusion.13 = f32[2,8,32,32]{3,2,1,0:T(8,128)S(1)} fusion(f32[8,128,2,2,32]{1,4,0,2,3:T(8,128)} %all-reduce.2.cloned.1.call-done, f32[8,128]{1,0:T(8,128)S(1)} %fusion.24), kind=kOutput, calls=%fused_computation.25 | convolution fusion | flops 25231360 | bytes 593920 | tf_op jit(solution)/shard_map/stli,stlj->lsij/dot_general | solution.py:64
  77.6 0.1 reshape.68
  77.7 14.7 %all_gather.10 = f32[2,64,1024]{2,1,0:T(8,128)S(1)} all-gather(f32[2,8,1024]{2,1,0:T(8,128)S(1)} %reshape.68), channel_id=1, replica_groups=mesh['dp'=8,'mp'=4] {'dp'}, dimensions={1}, use_global_device_ids=true | all-gather | bytes 589824 | tf_op jit(solution)/shard_map/all_gather | solution.py:69
  92.4 0.4 fusion.27
  92.9 0.8 fusion.8
  93.7 0.2 multiply_reduce_fusion
  93.9 0.7 fusion.19
  94.6 0.8 fusion.7
  95.4 0.7 convolution_bitcast_fusion
  96.1 8.1 %all-gather = f32[4,64,8]{1,2,0:T(8,128)S(1)} all-gather(f32[1,64,8]{1,2,0:T(8,128)S(1)} %convolution_bitcast_fusion), channel_id=1, replica_groups=mesh['dp'=8,'mp'=4] {'mp'}, dimensions={0}, use_global_device_ids=true | all-gather | bytes 10240 | tf_op jit(solution)/shard_map/all_gather | solution.py:85
  104.3 0.7 reshape.79
  (8 shorter events, 0.1 us)
Async XLA Ops:
  6.5 16.2 %copy-start = (bf16[1,1024,1024]{2,1,0:T(8,128)(2,1)S(1)}, bf16[1,1024,1024]{2,1,0:T(8,128)(2,1)}, u32[]{:S(2)}) copy-start(bf16[1,1024,1024]{2,1,0:T(8,128)(2,1)} %param.15) | copy-start | bytes 6291460
  6.5 69.5 %all-reduce.2.cloned.1.call-start = ((), (), s32[]{:S(2)}) async-start(), calls=%async_computation.1 | async-start | bytes 1048576 | tf_op jit(solution)/shard_map/psum | solution.py:59
  15.4 7.4 %copy-start.3 = (bf16[1,1024,32]{1,2,0:T(8,128)(2,1)S(1)}, bf16[1,1024,32]{1,2,0:T(8,128)(2,1)}, u32[]{:S(2)}) copy-start(bf16[1,1024,32]{1,2,0:T(8,128)(2,1)} %param.17) | copy-start | bytes 196612
  15.4 8.2 %copy-start.4 = (bf16[1,1024,32]{1,2,0:T(8,128)(2,1)S(1)}, bf16[1,1024,32]{1,2,0:T(8,128)(2,1)}, u32[]{:S(2)}) copy-start(bf16[1,1024,32]{1,2,0:T(8,128)(2,1)} %param.18) | copy-start | bytes 196612
  22.8 1.6 %copy-start.1 = (bf16[1,1024,1024]{2,1,0:T(8,128)(2,1)S(1)}, bf16[1,1024,1024]{2,1,0:T(8,128)(2,1)}, u32[]{:S(2)}) copy-start(bf16[1,1024,1024]{2,1,0:T(8,128)(2,1)} %param.16) | copy-start | bytes 6291460
  22.8 2.3 %copy-start.2 = (bf16[1024,1024]{1,0:T(8,128)(2,1)S(1)}, bf16[1024,1024]{1,0:T(8,128)(2,1)}, u32[]{:S(2)}) copy-start(bf16[1024,1024]{1,0:T(8,128)(2,1)} %param.12) | copy-start | bytes 6291460
  22.8 2.3 %copy-start.5 = (bf16[1024,32]{0,1:T(8,128)(2,1)S(1)}, bf16[1024,32]{0,1:T(8,128)(2,1)}, u32[]{:S(2)}) copy-start(bf16[1024,32]{0,1:T(8,128)(2,1)} %param.14) | copy-start | bytes 196612
  25.9 1.1 %copy-start.6 = (bf16[2,256,32]{1,2,0:T(8,128)(2,1)S(1)}, bf16[2,256,32]{1,2,0:T(8,128)(2,1)}, u32[]{:S(2)}) copy-start(bf16[2,256,32]{1,2,0:T(8,128)(2,1)} %param.19) | copy-start | bytes 98308
  25.9 21.9 %copy-start.7 = (s32[8]{0:T(128)S(1)}, s32[8]{0:T(128)}, u32[]{:S(2)}) copy-start(s32[8]{0:T(128)} %param.11) | copy-start | bytes 100
  44.0 9.6 %all-to-all-start = ((bf16[2,256,256]{1,0,2:T(2,128)(2,1)}), bf16[2,256,256]{1,0,2:T(2,128)(2,1)S(1)}, u32[]{:S(2)}, u32[]{:S(2)}) async-start(bf16[2,256,256]{1,0,2:T(2,128)(2,1)} %all_gather.9), calls=%async_computation | async-start | bytes 524288 | tf_op jit(solution)/shard_map/all_to_all | solution.py:70
Sparse Core Ops, SparseCore 0:
  27.1 48.8 all-reduce.1
where the time goes:
time: 112 us
  blocking collectives  39.8 us (36%)
  waiting for transfers between devices  27.3 us (24%)
  local copies, waits for them, and re-layouts  17.8 us (16%)
  between operations  13.6 us (12%)
  matrix products  7.11 us (6%)
  starting transfers between devices  3.71 us (3%)
  other arithmetic  2.52 us (2%)
    psum x1, waiting for transfers between devices, per_device(): summed = lax.psum(projected, 'mp')  21.5 us
    all_gather x1, blocking collectives, per_device(): targets = lax.all_gather(queries, 'dp', axis=2, tiled=True)  17 us
    all_gather x1, blocking collectives, per_device(): everyone = lax.all_gather(sketches, 'dp', axis=1, tiled=True)  14.7 us
    unnamed x20, local copies, waits for them, and re-layouts  8.96 us
    all_gather x1, blocking collectives, per_device(): scores = lax.all_gather(partial_value, 'mp', axis=1, tiled=True)  8.14 us
    gather x2, local copies, waits for them, and re-layouts, per_device(): jnp.take(vocab_basis, jnp.clip(local_ids, 0, vocab_rows - 1), axis=0)  7.42 us
    all_to_all x1, waiting for transfers between devices, per_device(): lax.all_to_all(targets, 'mp', split_axis=2, concat_axis=1, tiled=True)  5.79 us
    all_to_all x1, starting transfers between devices, per_device(): lax.all_to_all(targets, 'mp', split_axis=2, concat_axis=1, tiled=True)  3.71 us
  transfers between devices with their start and end apart: 2, of which 2 were waited for; matrix products, arithmetic and copies ran while one was open for 1% of the time, Pallas kernels for 0%

commit v1 on v0

--- a/solution.py
+++ b/solution.py
@@ -56,7 +56,7 @@
     pieces.append(jnp.dot(layer_inputs[0], input_basis[0], preferred_element_type=jnp.float32))
     projected = jnp.concatenate(pieces, axis=1)
     inverse_len = 1.0 / lengths.astype(jnp.float32)
-    summed = lax.psum(projected, "mp")
+    summed = lax.all_gather(projected, "mp").sum(axis=0)
     layout = summed.reshape(seq_count, slot_len, layer_count, 2, basis_rank)
     position = jnp.arange(slot_len, dtype=jnp.int32)
     weights = jnp.where(position[None, :] < lengths[:, None], inverse_len[:, None], 0.0)

time: 112 us -> 107 us (0.955)
  waiting for transfers between devices: 27.3 us -> 16.4 us
  other arithmetic: 2.52 us -> 6.2 us
  local copies, waits for them, and re-layouts: 17.8 us -> 20.6 us
    psum x1 -> x0, waiting for transfers between devices: 21.5 us -> none  [per_device(): summed = lax.psum(projected, 'mp')]
    all_gather x0 -> x1, waiting for transfers between devices: none -> 10.6 us  [per_device(): summed = lax.all_gather(projected, 'mp').sum(axis=0)]
    all_gather x0 -> x1, local copies, waits for them, and re-layouts: none -> 3.64 us  [per_device(): summed = lax.all_gather(projected, 'mp').sum(axis=0)]
    reduce_sum x0 -> x1, other arithmetic: none -> 2.86 us  [per_device(): summed = lax.all_gather(projected, 'mp').sum(axis=0)]
where the time goes in v1:
time: 107 us; the launch traced here: 106 us
  blocking collectives  39.8 us (37%)
  local copies, waits for them, and re-layouts  20.6 us (19%)
  waiting for transfers between devices  16.4 us (15%)
  between operations  13.6 us (13%)
  other arithmetic  6.2 us (6%)
  matrix products  6.13 us (6%)
  starting transfers between devices  3.71 us (3%)
    all_gather x1, blocking collectives, per_device(): targets = lax.all_gather(queries, 'dp', axis=2, tiled=True)  17 us
    all_gather x1, blocking collectives, per_device(): everyone = lax.all_gather(sketches, 'dp', axis=1, tiled=True)  14.8 us
    all_gather x1, waiting for transfers between devices, per_device(): summed = lax.all_gather(projected, 'mp').sum(axis=0)  10.6 us
    unnamed x20, local copies, waits for them, and re-layouts  8.97 us
    all_gather x1, blocking collectives, per_device(): scores = lax.all_gather(partial_value, 'mp', axis=1, tiled=True)  7.94 us
    gather x2, local copies, waits for them, and re-layouts, per_device(): jnp.take(vocab_basis, jnp.clip(local_ids, 0, vocab_rows - 1), axis=0)  7.42 us
    all_to_all x1, waiting for transfers between devices, per_device(): lax.all_to_all(targets, 'mp', split_axis=2, concat_axis=1, tiled=True)  5.79 us
    all_to_all x1, starting transfers between devices, per_device(): lax.all_to_all(targets, 'mp', split_axis=2, concat_axis=1, tiled=True)  3.71 us
  transfers between devices with their start and end apart: 2, of which 2 were waited for; matrix products, arithmetic and copies ran while one was open for 1% of the time, Pallas kernels for 0%

profile of v1, /device:TPU:0, one launch (start us, length us, event | category | flops | bytes accessed | tf_op | source)
XLA Modules:
  0.0 106.4 jit_solution(1835020389606034706)
XLA Ops:
  6.5 0.0 copy-start
  6.5 0.0 all-gather.4.cloned.1.call-start
  6.5 0.8 compare_and_fusion.1
  7.4 0.7 fusion.24
  8.1 7.3 %copy.31 = bf16[32064,32]{1,0:T(8,128)(2,1)} copy(bf16[32064,32]{0,1:T(8,128)(2,1)} %param.13) | data formatting | bytes 4104192 | tf_op args[3]
  15.4 0.0 copy-start.3
  15.4 7.3 %gather_fusion = bf16[1024,32]{1,0:T(8,128)(2,1)S(1)} fusion(bf16[32064,32]{1,0:T(8,128)(2,1)} %copy.31, s32[1024]{0:T(1024)S(1)} %fusion.24), kind=kCustom, calls=%fused_computation | custom fusion | bytes 135168 | tf_op jit(solution)/shard_map/jit(_take)/gather | solution.py:50
  22.7 0.1 copy.32
  22.8 0.0 copy-done
  22.8 0.0 copy-done.3
  22.8 0.0 copy-start.1
  22.8 0.0 copy-start.2
  22.8 0.0 copy-start.5
  22.8 0.7 fusion
  23.6 0.0 copy-done.4
  23.6 0.8 copy-done.1
  24.4 0.7 fusion.2
  25.1 0.0 copy-done.2
  25.1 0.0 copy-done.5
  25.1 0.0 copy-start.6
  25.1 0.0 copy-start.7
  25.2 0.7 fusion.25
  25.9 0.8 pad_maximum_fusion
  26.8 0.0 all-gather.4.cloned.1.call-update
  26.8 0.0 copy-done.6
  26.8 17.0 %all_gather.17 = bf16[2,256,256]{1,0,2:T(2,128)(2,1)} all-gather(bf16[2,256,32]{1,0,2:T(2,128)(2,1)S(1)} %copy.29), channel_id=1, replica_groups=mesh['dp'=8,'mp'=4] {'dp'}, dimensions={2}, use_global_device_ids=true | all-gather | bytes 294912 | tf_op jit(solution)/shard_map/all_gather | solution.py:68
  43.8 3.7 %all-to-all-start = ((bf16[2,256,256]{1,0,2:T(2,128)(2,1)}), bf16[2,256,256]{1,0,2:T(2,128)(2,1)S(1)}, u32[]{:S(2)}, u32[]{:S(2)}) async-start(bf16[2,256,256]{1,0,2:T(2,128)(2,1)} %all_gather.17), calls=%async_computation | async-start | bytes 524288 | tf_op jit(solution)/shard_map/all_to_all | solution.py:70
  47.5 0.0 copy-done.7
  47.5 0.1 fusion.23
  47.6 5.8 %all-to-all-done = bf16[2,256,256]{1,0,2:T(2,128)(2,1)S(1)} async-done(((bf16[2,256,256]{1,0,2:T(2,128)(2,1)}), bf16[2,256,256]{1,0,2:T(2,128)(2,1)S(1)}, u32[]{:S(2)}, u32[]{:S(2)}) %all-to-all-start) | async-done | bytes 262176 | tf_op jit(solution)/shard_map/all_to_all | solution.py:70
  53.4 0.2 copy.49
  53.6 0.2 all_to_all.16
  53.8 0.6 multiply_reduce_fusion.1
  54.4 10.6 %all-gather.4.cloned.1.call-done = f32[4096,128]{0,1:T(8,128)} async-done(((f32[1024,128]{0,1:T(8,128)}), f32[4096,128]{0,1:T(8,128)}) %all-gather.4.cloned.1.call-update) | async-done | bytes 2097168 | tf_op jit(solution)/shard_map/all_gather | solution.py:59
  64.9 3.6 %reshape.77 = f32[4,1024,128]{1,0,2:T(4,128)} reshape(f32[4096,128]{0,1:T(8,128)} %all-gather.4.cloned.1.call-done) | data formatting | bytes 4194304 | tf_op jit(solution)/shard_map/all_gather | solution.py:59
  68.6 2.9 %reduce_sum.45 = f32[1024,128]{0,1:T(8,128)S(1)} reduce(f32[4,1024,128]{1,0,2:T(4,128)} %reshape.77, f32[]{:T(128)} %constant.15.clone.1), dimensions={0}, to_apply=%region_0.1 | reduce | flops 393216 | bytes 2621444 | tf_op jit(solution)/shard_map/reduce_sum | solution.py:59
  71.4 0.1 copy.41
  71.6 0.6 fusion.14
  72.2 0.1 reshape.68
  72.3 14.8 %all_gather.18 = f32[2,64,1024]{2,1,0:T(8,128)S(1)} all-gather(f32[2,8,1024]{2,1,0:T(8,128)S(1)} %reshape.68), channel_id=1, replica_groups=mesh['dp'=8,'mp'=4] {'dp'}, dimensions={1}, use_global_device_ids=true | all-gather | bytes 589824 | tf_op jit(solution)/shard_map/all_gather | solution.py:69
  87.2 0.4 fusion.26
  87.6 0.8 fusion.8
  88.4 0.2 multiply_reduce_fusion
  88.6 0.7 fusion.19
  89.4 0.8 fusion.7
  90.2 0.7 convolution_bitcast_fusion
  90.9 7.9 %all-gather.1 = f32[4,64,8]{1,2,0:T(8,128)S(1)} all-gather(f32[1,64,8]{1,2,0:T(8,128)S(1)} %convolution_bitcast_fusion), channel_id=1, replica_groups=mesh['dp'=8,'mp'=4] {'mp'}, dimensions={0}, use_global_device_ids=true | all-gather | bytes 10240 | tf_op jit(solution)/shard_map/all_gather | solution.py:85
  98.8 0.7 reshape.80
  (10 shorter events, 0.1 us)
Async XLA Ops:
  6.5 16.2 %copy-start = (bf16[1,1024,1024]{2,1,0:T(8,128)(2,1)S(1)}, bf16[1,1024,1024]{2,1,0:T(8,128)(2,1)}, u32[]{:S(2)}) copy-start(bf16[1,1024,1024]{2,1,0:T(8,128)(2,1)} %param.15) | copy-start | bytes 6291460
  6.5 58.4 %all-gather.4.cloned.1.call-start = ((), (), s32[]{:S(2)}) async-start(), calls=%async_computation.1 | async-start | bytes 2621440 | tf_op jit(solution)/shard_map/all_gather | solution.py:59
  15.4 7.4 %copy-start.3 = (bf16[1,1024,32]{1,2,0:T(8,128)(2,1)S(1)}, bf16[1,1024,32]{1,2,0:T(8,128)(2,1)}, u32[]{:S(2)}) copy-start(bf16[1,1024,32]{1,2,0:T(8,128)(2,1)} %param.17) | copy-start | bytes 196612
  15.4 8.2 %copy-start.4 = (bf16[1,1024,32]{1,2,0:T(8,128)(2,1)S(1)}, bf16[1,1024,32]{1,2,0:T(8,128)(2,1)}, u32[]{:S(2)}) copy-start(bf16[1,1024,32]{1,2,0:T(8,128)(2,1)} %param.18) | copy-start | bytes 196612
  22.8 1.6 %copy-start.1 = (bf16[1,1024,1024]{2,1,0:T(8,128)(2,1)S(1)}, bf16[1,1024,1024]{2,1,0:T(8,128)(2,1)}, u32[]{:S(2)}) copy-start(bf16[1,1024,1024]{2,1,0:T(8,128)(2,1)} %param.16) | copy-start | bytes 6291460
  22.8 2.3 %copy-start.2 = (bf16[1024,1024]{1,0:T(8,128)(2,1)S(1)}, bf16[1024,1024]{1,0:T(8,128)(2,1)}, u32[]{:S(2)}) copy-start(bf16[1024,1024]{1,0:T(8,128)(2,1)} %param.12) | copy-start | bytes 6291460
  22.8 2.3 %copy-start.5 = (bf16[1024,32]{0,1:T(8,128)(2,1)S(1)}, bf16[1024,32]{0,1:T(8,128)(2,1)}, u32[]{:S(2)}) copy-start(bf16[1024,32]{0,1:T(8,128)(2,1)} %param.14) | copy-start | bytes 196612
  25.1 1.6 %copy-start.6 = (bf16[2,256,32]{1,2,0:T(8,128)(2,1)S(1)}, bf16[2,256,32]{1,2,0:T(8,128)(2,1)}, u32[]{:S(2)}) copy-start(bf16[2,256,32]{1,2,0:T(8,128)(2,1)} %param.19) | copy-start | bytes 98308
  25.1 22.4 %copy-start.7 = (s32[8]{0:T(128)S(1)}, s32[8]{0:T(128)}, u32[]{:S(2)}) copy-start(s32[8]{0:T(128)} %param.11) | copy-start | bytes 100
  43.8 9.6 %all-to-all-start = ((bf16[2,256,256]{1,0,2:T(2,128)(2,1)}), bf16[2,256,256]{1,0,2:T(2,128)(2,1)S(1)}, u32[]{:S(2)}, u32[]{:S(2)}) async-start(bf16[2,256,256]{1,0,2:T(2,128)(2,1)} %all_gather.17), calls=%async_computation | async-start | bytes 524288 | tf_op jit(solution)/shard_map/all_to_all | solution.py:70
Sparse Core Ops, SparseCore 0:
  26.9 38.0 all-gather.3
